TPU v7x, 32 devices: a whole 2x2x4 slice. The times are simulated.
32 devices in a mesh: shift: 16 (over z, x, core), row: 2 (over y).
Axes of the slice: x: 2, y: 2, z: 4, core: 2. Of those that a mesh axis runs over, the one named last changes fastest.
Arguments:
- solutions: bfloat16 [32, 2, 2048, 128], P('shift', None, 'row'), may hold values from -96 to 96
Outputs:
- moments: bfloat16 [2, 8, 2048, 128], P(None, None, ('row', 'shift'))
- gram_real: float32 [1024, 1024], replicated
- gram_imag: float32 [1024, 1024], replicated
All inputs are finite; a program needn't handle non-finite values.
Results may differ from a plain program's by a relative error of at most 0.0061.
Values may be sent and summed in bfloat16 or wider, within the bound.
A program may use at most 64 MiB of HBM per device.

v0:
```python
import functools
import math

import jax
import jax.numpy as jnp
import numpy as np
from jax import lax
from jax.experimental import pallas as pl
from jax.experimental.pallas import tpu as pltpu
from jax.sharding import PartitionSpec as P

PANELS = 8
PAIRS = PANELS * (PANELS // 2) + PANELS // 2
UNITS = 2 * PAIRS
HALVES = 2
MESH = pl.DeviceIdType.MESH


def coefficients(all_shifts):
    indices = np.arange(all_shifts, dtype=np.float32)
    orders = np.arange(1, PANELS + 1, dtype=np.float32)
    step = (np.float32(2.0 * math.pi) * (indices + np.float32(0.5)) / np.float32(all_shifts)).astype(np.float32)
    angles = (orders[:, None] * step[None, :]).astype(np.float32).astype(np.float64)
    cos_part = np.cos(angles).astype(np.float32) / np.float32(all_shifts)
    sin_part = np.sin(angles).astype(np.float32) / np.float32(all_shifts)
    real_row = np.stack([cos_part, -sin_part], axis=-1)
    imag_row = np.stack([sin_part, cos_part], axis=-1)
    both = np.stack([real_row, imag_row], axis=0).reshape(-1)
    return both.astype(jnp.bfloat16).astype(np.float32)


def exchange(
    N, R, rows, T, factor,
    w_ref, x_ref, m_ref, ag, xs, acc, sbuf, gs, rs,
    a2a_s, a2a_r, sg_s, sg_r, rs_s, rs_r, ag_s, ag_r,
):
    Z = N // 4
    s = lax.axis_index("shift")
    r = lax.axis_index("row")
    core = lax.rem(s, 2)
    z = s // 4
    x = lax.rem(s // 2, 2)
    inputs = x_ref.shape[0]
    outs = 2 * PANELS
    part = rows // HALVES

    def member(x_, r_, c_):
        return (r_ * 2 + x_) * 2 + c_

    def place(z_, x_, c_):
        return (z_ * 2 + x_) * 2 + c_

    p = member(x, r, core)
    partner = place(z, x, 1 - core)
    across = place(z, 1 - x, core)

    def row_at(i):
        return lax.rem(r + i + R, R)

    def remote(src, dst, ss, rr, to_s, to_r):
        return pltpu.make_async_remote_copy(
            src_ref=src, dst_ref=dst, send_sem=ss, recv_sem=rr,
            device_id={"shift": to_s, "row": to_r}, device_id_type=MESH,
        )

    barrier = pltpu.get_barrier_semaphore()
    for i in range(1, N):
        pl.semaphore_signal(barrier, inc=1, device_id={"shift": lax.rem(s + i, N), "row": r}, device_id_type=MESH)
    for i in range(1, R):
        pl.semaphore_signal(barrier, inc=1, device_id={"shift": s, "row": row_at(i)}, device_id_type=MESH)
    pl.semaphore_wait(barrier, N - 1 + R - 1)

    def a2a(h, i):
        to = lax.rem(s + i, N)
        return remote(
            x_ref.at[:, pl.ds(pl.multiple_of(to * rows + h * part, part), part), :], xs.at[h, i],
            a2a_s.at[h, i], a2a_r.at[h, i], to, r,
        )

    def order(j):
        return 1 + j

    def send_one(j, c):
        a2a(j // (N - 1), order(lax.rem(j, N - 1))).start()
        return c

    lax.fori_loop(0, HALVES * (N - 1), send_one, 0)

    strip = 16 if part % 16 == 0 else part

    def weigh(block, source, first):
        for b in range(part // strip):
            at = slice(b * strip, (b + 1) * strip)
            parts = [block(c, at).astype(jnp.float32) for c in range(inputs)]
            for o in range(outs):
                base = o * inputs * N + source * inputs
                total = parts[0] * w_ref[base]
                for c in range(1, inputs):
                    total += parts[c] * w_ref[base + c]
                if first:
                    acc[o, at, :] = total
                else:
                    acc[o, at, :] += total

    def take(h, low, high):
        def take_one(j, c):
            i = order(j)
            a2a(h, i).wait_recv()
            weigh(lambda q, at: xs[h, i, q, at, :], lax.rem(s - i + N, N), False)
            return c

        lax.fori_loop(low, high, take_one, 0)

    def own(h):
        weigh(
            lambda c, at: x_ref[c, pl.ds(pl.multiple_of(s * rows + h * part + at.start, strip), strip), :],
            s, True,
        )

    def round_all(h):
        def round_one(o, c):
            value = acc[o].astype(jnp.bfloat16)
            sbuf[h, p, o] = value
            m_ref[o, h * part : (h + 1) * part, :] = value
            return c

        lax.fori_loop(0, outs, round_one, 0)

    done = []

    def spreader(view, send_sems, recv_sems):
        count = [0]

        def copy(at, slot, to_s, to_r):
            return remote(view(at, slot), view(at, slot), send_sems.at[count[0]], recv_sems.at[at, slot], to_s, to_r)

        def forward(at, slot, to_s, to_r):
            c = copy(at, slot, to_s, to_r)
            count[0] += 1
            c.start()
            done.append(c)

        def arrive(at, slot):
            remote(view(at, slot), view(at, slot), send_sems.at[0], recv_sems.at[at, slot], s, r).wait_recv()

        def spread(at):
            forward(at, p, across, r)
            for i in range(1, R):
                forward(at, p, s, row_at(i))
            forward(at, p, partner, r)

        def relay(at):
            arrive(at, member(1 - x, r, core))
            for i in range(1, R):
                arrive(at, member(x, row_at(-i), core))
            for i in range(1, R):
                first = core == 0
                slot = jnp.where(first, member(1 - x, r, core), member(x, row_at(-i), core))
                forward(at, slot, jnp.where(first, s, across), jnp.where(first, row_at(i), r))
            forward(at, member(1 - x, r, core), partner, r)
            for i in range(1, R):
                forward(at, member(x, row_at(-i), core), partner, r)

        def diagonal(at):
            for i in range(1, R):
                slot = member(1 - x, row_at(-i), core)
                arrive(at, slot)
                forward(at, slot, partner, r)

        def rest(at):
            for i in range(R):
                for o in range(2):
                    arrive(at, member(lax.rem(x + o, 2), row_at(i), 1 - core))

        return spread, relay, diagonal, rest, arrive, forward

    spread, relay, diagonal, rest, _, _ = spreader(lambda h, slot: sbuf.at[h, slot], sg_s, sg_r)
    for h in range(HALVES):
        own(h)
        if h == 0:
            take(h, 0, N - 1)
        else:
            mid = (2 * (N - 1)) // 3
            take(h, 0, mid)
            relay(h - 1)
            take(h, mid, N - 1)
        round_all(h)
        spread(h)
        if h > 0:
            diagonal(h - 1)
    relay(HALVES - 1)
    diagonal(HALVES - 1)
    for h in range(HALVES):
        rest(h)

    depth = 4 * R * rows
    first_pair = (p * T) // 2
    odd = lax.rem(p * T, 2)

    def pair_one(j, c):
        u = jnp.minimum(first_pair + j, PAIRS - 1)
        k = lax.rem(u, PANELS)
        q = lax.rem(k + u // PANELS, PANELS)
        lr = sbuf[:, :, k].reshape(depth, -1)
        li = sbuf[:, :, PANELS + k].reshape(depth, -1)
        rr = sbuf[:, :, q].reshape(depth, -1)
        ri = sbuf[:, :, PANELS + q].reshape(depth, -1)
        dims = (((0,), (0,)), ((), ()))
        out = lax.dot_general(
            lr, jnp.concatenate([rr, ri], axis=1), dims, preferred_element_type=jnp.float32
        ) + lax.dot_general(
            li, jnp.concatenate([ri, -rr], axis=1), dims, preferred_element_type=jnp.float32
        )
        out = (out * factor).astype(jnp.bfloat16)
        cut = out.shape[0] // (2 * Z)
        for half in range(2):
            for m in range(Z):
                n = half * Z + m
                gs[m, 2 * j + half + 1 - odd] = out[n * cut : (n + 1) * cut]
        return c

    lax.fori_loop(0, (T + 2) // 2 if T % 2 else T // 2, pair_one, 0)

    def reduce(i):
        to = lax.rem(z + i, Z)
        return remote(gs.at[to, pl.ds(1, T)], rs.at[i], rs_s.at[i], rs_r.at[i], place(to, x, core), r)

    for j in range(Z - 1):
        c = reduce(1 + (Z // 2 - 1 + j) % (Z - 1))
        c.start()
        done.append(c)
    for i in range(1, Z):
        reduce(i).wait_recv()

    def sum_one(t, c):
        total = gs[z, t + 1].astype(jnp.float32)
        for i in range(1, Z):
            total += rs[i, t].astype(jnp.float32)
        ag[p, z, t] = total.astype(jnp.bfloat16)
        return c

    lax.fori_loop(0, T, sum_one, 0)

    spread, relay, diagonal, rest, arrive, forward = spreader(lambda at, slot: ag.at[slot, at], ag_s, ag_r)
    def mate(m):
        if Z & (Z - 1):
            return lax.rem(z + m, Z), lax.rem(z + Z - m, Z)
        out = z
        for b in range(m.bit_length()):
            if m >> b & 1:
                out = out + (1 - 2 * lax.rem(z // (1 << b), 2)) * (1 << b)
        return out, out

    for m in range(1, Z):
        forward(z, p, place(mate(m)[0], x, core), r)
    ats = [z] + [mate(m)[1] for m in range(1, Z)]
    for n in range(Z + 2):
        if n < Z:
            if n > 0:
                arrive(ats[n], p)
            spread(ats[n])
        if 0 <= n - 1 < Z:
            relay(ats[n - 1])
        if 0 <= n - 2 < Z:
            diagonal(ats[n - 2])
    for at in ats:
        rest(at)

    def drain(j, c):
        a2a(j // (N - 1), order(lax.rem(j, N - 1))).wait_send()
        return c

    lax.fori_loop(0, HALVES * (N - 1), drain, 0)
    for c in done:
        c.wait_send()


def expand(T, m_in, ag_ref, m_out, re_out, im_out, re_buf, im_buf, sems, m_sem):
    width = re_buf.shape[1]
    half = PANELS // 2
    keep = pltpu.make_async_copy(m_in, m_out, m_sem)
    keep.start()

    def unit(n):
        return ag_ref[n // T, :, lax.rem(n, T)].astype(jnp.float32).reshape(width // 2, 2 * width)

    def pair(u):
        return jnp.concatenate([unit(2 * u), unit(2 * u + 1)], axis=0)

    def writes(k, slot):
        at = pl.ds(pl.multiple_of(k * width, width), width)
        return (
            pltpu.make_async_copy(re_buf.at[k], re_out.at[at], sems.at[0, k]),
            pltpu.make_async_copy(im_buf.at[k], im_out.at[at], sems.at[1, k]),
        )

    def one(k, c):
        for d in range(PANELS):
            q = lax.rem(k + d, PANELS)
            at = pl.ds(pl.multiple_of(q * width, width), width)
            if d < half:
                v = pair(PANELS * d + k)
                re, im = v[:, :width], v[:, width:]
            elif d == half:
                v = pair(PANELS * half + jnp.minimum(k, q))
                re, im = v[:, :width], v[:, width:]
                re, im = jnp.where(k < half, re, re.T), jnp.where(k < half, im, -im.T)
            else:
                v = pair(PANELS * (PANELS - d) + q)
                re, im = v[:, :width].T, -v[:, width:].T
            re_buf[k, :, at] = re
            im_buf[k, :, at] = im
        for copy in writes(k, k):
            copy.start()
        return c

    lax.fori_loop(0, PANELS, one, 0)

    def finish(k, c):
        for copy in writes(k, k):
            copy.wait()
        return c

    lax.fori_loop(0, PANELS, finish, 0)
    keep.wait()


def local(N, R, solutions):
    shifts, parts, height, width = solutions.shape
    rows = height // N
    Z = N // 4
    G = 4 * R
    T = -(-UNITS // G)
    cut = width // (2 * Z)
    inputs = shifts * parts
    outs = 2 * PANELS
    part = rows // HALVES
    factor = 1.0 / math.sqrt(height * R)
    w = jnp.asarray(coefficients(shifts * N))
    bf, dma = jnp.bfloat16, pltpu.SemaphoreType.DMA
    shared = 4 * R
    vmem = pl.BlockSpec(memory_space=pltpu.VMEM)
    moments, parts_of_gram = pl.pallas_call(
        functools.partial(exchange, N, R, rows, T, factor),
        out_shape=(
            jax.ShapeDtypeStruct((outs, rows, width), bf),
            jax.ShapeDtypeStruct((G, Z, T, cut, 2 * width), bf),
        ),
        in_specs=[pl.BlockSpec(memory_space=pltpu.SMEM), vmem],
        out_specs=(vmem, vmem),
        scratch_shapes=[
            pltpu.VMEM((HALVES, N, inputs, part, width), bf),
            pltpu.VMEM((outs, part, width), jnp.float32),
            pltpu.VMEM((HALVES, G, outs, part, width), bf),
            pltpu.VMEM((Z, T + 2, cut, 2 * width), bf),
            pltpu.VMEM((Z, T, cut, 2 * width), bf),
            dma((HALVES, N)), dma((HALVES, N)), dma((HALVES * shared,)), dma((HALVES, G)),
            dma((Z,)), dma((Z,)), dma((Z * shared + Z,)), dma((Z, G)),
        ],
        compiler_params=pltpu.CompilerParams(
            collective_id=0, has_side_effects=True, vmem_limit_bytes=32 * 2**20
        ),
        cost_estimate=pl.CostEstimate(flops=10**9, bytes_accessed=2**23, transcendentals=0),
    )(w, solutions.reshape(inputs, height, width))
    size = PANELS * width
    anywhere = pl.BlockSpec(memory_space=pl.ANY)
    moments, gram_real, gram_imag = pl.pallas_call(
        functools.partial(expand, T),
        out_shape=(
            jax.ShapeDtypeStruct((outs, rows, width), bf),
            jax.ShapeDtypeStruct((size, size), jnp.float32),
            jax.ShapeDtypeStruct((size, size), jnp.float32),
        ),
        in_specs=[vmem, vmem],
        out_specs=(anywhere, anywhere, anywhere),
        scratch_shapes=[
            pltpu.VMEM((PANELS, width, size), jnp.float32),
            pltpu.VMEM((PANELS, width, size), jnp.float32),
            dma((2, PANELS)),
            dma,
        ],
        compiler_params=pltpu.CompilerParams(vmem_limit_bytes=32 * 2**20),
        cost_estimate=pl.CostEstimate(flops=10**7, bytes_accessed=2**24, transcendentals=0),
    )(moments, parts_of_gram)
    return moments.reshape(2, PANELS, rows, width), gram_real, gram_imag


def solution(mesh):
    return jax.shard_map(
        functools.partial(local, mesh.shape["shift"], mesh.shape["row"]),
        mesh=mesh,
        in_specs=(P("shift", None, "row", None),),
        out_specs=(P(None, None, ("row", "shift"), None), P(), P()),
        check_vma=False,
    )
```

profile of v0, /device:TPU:0, one launch (start us, length us, event | category | flops | bytes accessed | tf_op | source)
XLA Modules:
  0.0 75.7 jit_solution(9819543015635131897)
XLA Ops:
  0.6 0.0 copy-start
  0.6 1.2 %copy-done = bf16[2,2,1024,128]{3,2,1,0:T(8,128)(2,1)S(1)} copy-done((bf16[2,2,1024,128]{3,2,1,0:T(8,128)(2,1)S(1)}, bf16[2,2,1024,128]{3,2,1,0:T(8,128)(2,1)}, u32[]{:S(2)}) %copy-start) | copy-done | bytes 1048600
  1.9 0.0 copy-start.1
  1.9 0.7 copy-done.1
  2.5 69.4 %shard_map.49 = (bf16[16,64,128]{2,1,0:T(8,128)(2,1)S(1)}, bf16[8,4,9,16,256]{4,3,2,1,0:T(8,128)(2,1)S(1)}) custom-call(f32[1024]{0:T(1024)S(1)} %copy-done.1, bf16[4,1024,128]{2,1,0:T(8,128)(2,1)S(1)} %bitcast.2), custom_call_target="tpu_custom_call" | custom-call | flops 1000000000 | bytes 8388608 | tf_op jit(solution)/shard_map/pallas_call | solution.py:343
  72.0 3.7 %shard_map.50 = (bf16[16,64,128]{2,1,0:T(8,128)(2,1)}, f32[1024,1024]{1,0:T(8,128)}, f32[1024,1024]{1,0:T(8,128)}) custom-call(bf16[16,64,128]{2,1,0:T(8,128)(2,1)S(1)} %get-tuple-element.8.m_in, bf16[8,4,9,16,256]{4,3,2,1,0:T(8,128)(2,1)S(1)} %get-tuple-element.9.ag_ref), custom_call_target="tpu_custom_call" | custom-call | flops 10000000 | bytes 16777216 | tf_op jit(solution)/shard_map/pallas_call | solution.py:367
Async XLA Ops:
  0.6 1.2 %copy-start = (bf16[2,2,1024,128]{3,2,1,0:T(8,128)(2,1)S(1)}, bf16[2,2,1024,128]{3,2,1,0:T(8,128)(2,1)}, u32[]{:S(2)}) copy-start(bf16[2,2,1024,128]{3,2,1,0:T(8,128)(2,1)} %param.2) | copy-start | bytes 3145732
  1.9 0.7 copy-start.1
where the time goes:
time: 76.2 us; the launch traced here: 75.7 us
  Pallas kernels  73.1 us (96%)
  local copies, waits for them, and re-layouts  1.9 us (2%)
    pallas_call x1, Pallas kernels, local(): pl.pallas_call(functools.partial(exchange, N, R, rows, T, factor), out_sh...  69.4 us
    pallas_call x1, Pallas kernels, local(): pl.pallas_call(functools.partial(expand, T), out_shape=(jax.ShapeDtypeStr...  3.67 us
    unnamed x4, local copies, waits for them, and re-layouts  1.9 us

commit v1 on v0

v1 whole, which is shorter than its diff:
```python
import functools
import math

import jax
import jax.numpy as jnp
import numpy as np
from jax import lax
from jax.experimental import pallas as pl
from jax.experimental.pallas import tpu as pltpu
from jax.sharding import PartitionSpec as P

PANELS = 8
PAIRS = PANELS * (PANELS // 2) + PANELS // 2
OUTS = 2 * PANELS
RELAY_LAG = 4
DIAGONAL_LAG = 7
MESH = pl.DeviceIdType.MESH


def coefficients(all_shifts, owners):
    indices = np.arange(all_shifts, dtype=np.float32)
    orders = np.arange(1, PANELS + 1, dtype=np.float32)
    step = (np.float32(2.0 * math.pi) * (indices + np.float32(0.5)) / np.float32(all_shifts)).astype(np.float32)
    angles = (orders[:, None] * step[None, :]).astype(np.float32).astype(np.float64)
    cos_part = np.cos(angles).astype(np.float32) / np.float32(all_shifts)
    sin_part = np.sin(angles).astype(np.float32) / np.float32(all_shifts)
    real_row = np.stack([cos_part, -sin_part], axis=-1)
    imag_row = np.stack([sin_part, cos_part], axis=-1)
    both = np.stack([real_row, imag_row], axis=0).reshape(OUTS, owners, -1)
    return both.transpose(1, 0, 2).reshape(-1).astype(jnp.bfloat16).astype(np.float32)


def units_per_core(R):
    t = -(-2 * PAIRS // (4 * R))
    return t + 1 - t % 2


def exchange(
    N, R, rows, part, T, factor,
    w_hbm, x_hbm, m_ref, ag,
    w_ref, x_ref, xs, sbuf, own, dout, din, fo, up, fm,
    in_sems, a2a_s, a2a_r, sg_s, sg_r, dd_s, dd_r, up_s, fo_r, out_s, in_r, ag_s, ag_r,
):
    Z = N // 4
    CH = rows // part
    s = lax.axis_index("shift")
    r = lax.axis_index("row")
    core = lax.rem(s, 2)
    z = s // 4
    x = lax.rem(s // 2, 2)
    inputs = x_ref.shape[0]
    width = x_ref.shape[2]
    cut = width // 2
    slots = 2 * R

    def member(x_, r_, c_):
        return (r_ * 2 + x_) * 2 + c_

    def place(z_, x_, c_):
        return (z_ * 2 + x_) * 2 + c_

    p = member(x, r, core)
    here = r * 2 + x
    partner = place(z, x, 1 - core)
    across = place(z, 1 - x, core)

    def row_at(i):
        return lax.rem(r + i + R, R)

    def remote(src, dst, ss, rr, to_s, to_r):
        return pltpu.make_async_remote_copy(
            src_ref=src, dst_ref=dst, send_sem=ss, recv_sem=rr,
            device_id={"shift": to_s, "row": to_r}, device_id_type=MESH,
        )

    load_x = pltpu.make_async_copy(x_hbm, x_ref, in_sems.at[0])
    load_w = pltpu.make_async_copy(w_hbm, w_ref, in_sems.at[1])
    load_x.start()
    load_w.start()
    barrier = pltpu.get_barrier_semaphore()
    for i in range(1, N):
        pl.semaphore_signal(barrier, inc=1, device_id={"shift": lax.rem(s + i, N), "row": r}, device_id_type=MESH)
    for i in range(1, R):
        for to in (s, across):
            pl.semaphore_signal(barrier, inc=1, device_id={"shift": to, "row": row_at(i)}, device_id_type=MESH)
    load_x.wait()
    load_w.wait()
    pl.semaphore_wait(barrier, N - 1 + 2 * (R - 1))


    def rows_of(owner, h):
        return pl.ds(pl.multiple_of(owner * rows + h * part, part), part)

    def a2a_send(h, to):
        return remote(x_ref.at[:, rows_of(to, h), :], xs.at[h, s], a2a_s.at[h, to], a2a_r.at[h, s], to, r)

    def a2a_arrive(h, source):
        remote(xs.at[h, source], xs.at[h, source], a2a_s.at[h, source], a2a_r.at[h, source], s, r).wait_recv()

    for e in range(Z // 2):
        def send_chunk(h, c, e=e):
            for to_z in (e, Z - 1 - e):
                for dx, dc in ((0, 0), (1, 0), (0, 1), (1, 1)):
                    to = place(to_z, lax.rem(x + dx, 2), lax.rem(core + dc, 2))
                    if dx or dc:
                        a2a_send(h, to).start()
                    else:
                        @pl.when(to_z != z)
                        def _():
                            a2a_send(h, to).start()
            return c

        lax.fori_loop(0, CH, send_chunk, 0)


    def weigh(acc, blocks, source):
        parts = [b.astype(jnp.float32) for b in blocks]
        out = []
        for o in range(OUTS):
            base = (source * OUTS + o) * inputs
            total = parts[0] * w_ref[base]
            for c in range(1, inputs):
                total += parts[c] * w_ref[base + c]
            out.append(total if acc is None else acc[o] + total)
        return tuple(out)

    def gather(h, to_x, to_r):
        k = lax.rem(to_r - r + R, R) * 2 + lax.rem(to_x + x, 2)
        return remote(
            sbuf.at[h, here], sbuf.at[h, here], sg_s.at[h, k], sg_r.at[h, here], place(z, to_x, core), to_r,
        )

    peers = [(i, j) for i in range(R) for j in range(2) if i or j]

    def moments_of(h, c):
        acc = weigh(None, [x_ref[q, rows_of(s, h), :] for q in range(inputs)], s)

        def take(j, acc):
            source = lax.rem(s - 1 - j + N, N)
            a2a_arrive(h, source)
            return weigh(acc, [xs[h, source, q] for q in range(inputs)], source)

        acc = lax.fori_loop(0, N - 1, take, acc)
        at = pl.ds(pl.multiple_of(h * part, part), part)
        for o in range(OUTS):
            value = acc[o].astype(jnp.bfloat16)
            sbuf[h, here, o] = value
            m_ref[o, at, :] = value
        for i, j in peers:
            gather(h, lax.rem(x + j, 2), row_at(i)).start()
        return c

    lax.fori_loop(0, CH, moments_of, 0)

    def gathered(h, c):
        for i, j in peers:
            slot = row_at(i) * 2 + lax.rem(x + j, 2)
            remote(sbuf.at[h, slot], sbuf.at[h, slot], sg_s.at[h, 0], sg_r.at[h, slot], s, r).wait_recv()
        return c

    lax.fori_loop(0, CH, gathered, 0)


    depth = slots * rows
    middle = T // 2
    toward = 1 - 2 * core
    dims = (((0,), (0,)), ((), ()))

    def pair(j):
        u = jnp.minimum(here * T + j, PAIRS - 1)
        k = lax.rem(u, PANELS)
        q = lax.rem(k + u // PANELS, PANELS)
        lr = sbuf[:, :, k].reshape(depth, width)
        li = sbuf[:, :, PANELS + k].reshape(depth, width)
        rr = sbuf[:, :, q].reshape(depth, width)
        ri = sbuf[:, :, PANELS + q].reshape(depth, width)
        out = lax.dot_general(
            lr, jnp.concatenate([rr, ri], axis=1), dims, preferred_element_type=jnp.float32
        ) + lax.dot_general(
            li, jnp.concatenate([ri, -rr], axis=1), dims, preferred_element_type=jnp.float32
        )
        out = out * factor
        return out[:cut], out[cut:]

    def pick(a, b):
        return jnp.where(core == 0, a, b)

    def swap(t):
        return remote(dout.at[t], din.at[t], dd_s.at[t], dd_r.at[t], partner, r)

    low, high = pair(middle)
    dout[0] = pick(high, low).astype(jnp.bfloat16)
    own[0] = pick(low, high)
    swap(0).start()

    def theirs(n, c):
        low, high = pair(middle + toward * (n + 1))
        dout[2 * n + 1] = pick(low, high).astype(jnp.bfloat16)
        dout[2 * n + 2] = pick(high, low).astype(jnp.bfloat16)
        swap(2 * n + 1).start()
        swap(2 * n + 2).start()
        return c

    lax.fori_loop(0, middle, theirs, 0)

    def mine(n, c):
        low, high = pair(middle - toward * (n + 1))
        own[2 * n + 1] = pick(high, low)
        own[2 * n + 2] = pick(low, high)
        return c

    lax.fori_loop(0, middle, mine, 0)


    lower = z < Z // 2
    inner = jnp.where(lower, z + 1, z - 1)
    outer = jnp.where(lower, z - 1, z + 1)
    from_end = jnp.where(lower, z, Z - 1 - z)
    is_middle = from_end == Z // 2 - 1
    has_outer = from_end > 0
    inner_s = place(inner, x, core)
    outer_s = place(jnp.where(has_outer, outer, inner), x, core)

    def to_mate(t):
        return remote(up.at[t], fm.at[t], up_s.at[t], in_r.at[t], inner_s, r)

    def to_inner(t):
        return remote(up.at[t], fo.at[t], up_s.at[t], fo_r.at[t], inner_s, r)

    def to_outer(t):
        return remote(ag.at[p, t], ag.at[p, t], out_s.at[t], in_r.at[t], outer_s, r)

    def climb(t, c):
        swap(t).wait_recv()
        own[t] = own[t] + din[t].astype(jnp.float32)

        @pl.when(has_outer)
        def _():
            remote(fo.at[t], fo.at[t], up_s.at[t], fo_r.at[t], s, r).wait_recv()
            own[t] = own[t] + fo[t].astype(jnp.float32)

        up[t] = own[t].astype(jnp.bfloat16)

        @pl.when(is_middle)
        def _():
            to_mate(t).start()

        @pl.when(jnp.logical_not(is_middle))
        def _():
            to_inner(t).start()

        return c

    lax.fori_loop(0, T, climb, 0)


    counts = [0]
    done = []

    def copy(t, slot, ss, to_s, to_r):
        return remote(ag.at[slot, t], ag.at[slot, t], ss, ag_r.at[t, slot], to_s, to_r)

    def forward(t, slot, to_s, to_r):
        c = copy(t, slot, ag_s.at[counts[0]], to_s, to_r)
        counts[0] += 1
        c.start()
        done.append(c)

    def arrive(t, slot):
        copy(t, slot, ag_s.at[0], s, r).wait_recv()

    def total(t):
        @pl.when(is_middle)
        def _():
            remote(fm.at[t], fm.at[t], up_s.at[t], in_r.at[t], s, r).wait_recv()
            ag[p, t] = (up[t].astype(jnp.float32) + fm[t].astype(jnp.float32)).astype(jnp.bfloat16)

        @pl.when(jnp.logical_not(is_middle))
        def _():
            remote(ag.at[p, t], ag.at[p, t], up_s.at[t], in_r.at[t], s, r).wait_recv()

        @pl.when(has_outer)
        def _():
            to_outer(t).start()

    def spread(t):
        forward(t, p, across, r)
        for i in range(1, R):
            forward(t, p, s, row_at(i))
        forward(t, p, partner, r)

    def relay(t):
        arrive(t, member(1 - x, r, core))
        for i in range(1, R):
            arrive(t, member(x, row_at(-i), core))
        first = core == 0
        for i in range(1, R):
            slot = jnp.where(first, member(1 - x, r, core), member(x, row_at(-i), core))
            forward(t, slot, jnp.where(first, s, across), jnp.where(first, row_at(i), r))
        forward(t, member(1 - x, r, core), partner, r)
        for i in range(1, R):
            forward(t, member(x, row_at(-i), core), partner, r)

    def diagonal(t):
        for i in range(1, R):
            slot = member(1 - x, row_at(-i), core)
            arrive(t, slot)
            forward(t, slot, partner, r)

    def rest(t):
        for i in range(R):
            for o in range(2):
                arrive(t, member(lax.rem(x + o, 2), row_at(i), 1 - core))

    for n in range(T + DIAGONAL_LAG):
        if n < T:
            total(n)
            spread(n)
        if 0 <= n - RELAY_LAG < T:
            relay(n - RELAY_LAG)
        if 0 <= n - DIAGONAL_LAG < T:
            diagonal(n - DIAGONAL_LAG)
    for t in range(T):
        rest(t)


    def drain(h, c):
        for i in range(1, N):
            a2a_send(h, lax.rem(s + i, N)).wait_send()
        for i, j in peers:
            gather(h, lax.rem(x + j, 2), row_at(i)).wait_send()
        return c

    lax.fori_loop(0, CH, drain, 0)

    def drain_units(t, c):
        swap(t).wait_send()
        to_inner(t).wait_send()

        @pl.when(has_outer)
        def _():
            to_outer(t).wait_send()

        return c

    lax.fori_loop(0, T, drain_units, 0)
    for c in done:
        c.wait_send()


def expand(T, m_in, ag_ref, m_out, re_out, im_out, re_buf, im_buf, sems, m_sem):
    width = re_buf.shape[1]
    half = PANELS // 2
    keep = pltpu.make_async_copy(m_in, m_out, m_sem)
    keep.start()

    def unit(n):
        chip = n // (2 * T)
        v = lax.rem(n, 2 * T)
        low = v < T
        value = ag_ref[2 * chip + jnp.where(low, 0, 1), jnp.where(low, T - 1 - v, v - T)]
        return value.astype(jnp.float32)

    def pair(u):
        return jnp.concatenate([unit(2 * u), unit(2 * u + 1)], axis=0)

    def writes(k, slot):
        at = pl.ds(pl.multiple_of(k * width, width), width)
        return (
            pltpu.make_async_copy(re_buf.at[k], re_out.at[at], sems.at[0, k]),
            pltpu.make_async_copy(im_buf.at[k], im_out.at[at], sems.at[1, k]),
        )

    def one(k, c):
        for d in range(PANELS):
            q = lax.rem(k + d, PANELS)
            at = pl.ds(pl.multiple_of(q * width, width), width)
            if d < half:
                v = pair(PANELS * d + k)
                re, im = v[:, :width], v[:, width:]
            elif d == half:
                v = pair(PANELS * half + jnp.minimum(k, q))
                re, im = v[:, :width], v[:, width:]
                re, im = jnp.where(k < half, re, re.T), jnp.where(k < half, im, -im.T)
            else:
                v = pair(PANELS * (PANELS - d) + q)
                re, im = v[:, :width].T, -v[:, width:].T
            re_buf[k, :, at] = re
            im_buf[k, :, at] = im
        for copy in writes(k, k):
            copy.start()
        return c

    lax.fori_loop(0, PANELS, one, 0)

    def finish(k, c):
        for copy in writes(k, k):
            copy.wait()
        return c

    lax.fori_loop(0, PANELS, finish, 0)
    keep.wait()


def local(N, R, solutions):
    shifts, parts, height, width = solutions.shape
    rows = height // N
    T = units_per_core(R)
    G = 4 * R
    cut = width // 2
    inputs = shifts * parts
    part = 16 if rows % 16 == 0 else rows
    chunks = rows // part
    factor = 1.0 / math.sqrt(height * R)
    w = jnp.asarray(coefficients(shifts * N, N))
    bf, dma = jnp.bfloat16, pltpu.SemaphoreType.DMA
    vmem = pl.BlockSpec(memory_space=pltpu.VMEM)
    hbm = pl.BlockSpec(memory_space=pltpu.HBM)
    unit = (T, cut, 2 * width)
    spreads = T * (1 + (R - 1) + 1 + (R - 1) + 1 + (R - 1) + (R - 1))
    moments, parts_of_gram = pl.pallas_call(
        functools.partial(exchange, N, R, rows, part, T, factor),
        out_shape=(
            jax.ShapeDtypeStruct((OUTS, rows, width), bf),
            jax.ShapeDtypeStruct((G,) + unit, bf),
        ),
        in_specs=[hbm, hbm],
        out_specs=(vmem, vmem),
        scratch_shapes=[
            pltpu.SMEM(w.shape, jnp.float32),
            pltpu.VMEM((inputs, height, width), bf),
            pltpu.VMEM((chunks, N, inputs, part, width), bf),
            pltpu.VMEM((chunks, 2 * R, OUTS, part, width), bf),
            pltpu.VMEM(unit, jnp.float32),
            pltpu.VMEM(unit, bf), pltpu.VMEM(unit, bf), pltpu.VMEM(unit, bf),
            pltpu.VMEM(unit, bf), pltpu.VMEM(unit, bf),
            dma((2,)),
            dma((chunks, N)), dma((chunks, N)), dma((chunks, 2 * R)), dma((chunks, 2 * R)),
            dma((T,)), dma((T,)), dma((T,)), dma((T,)), dma((T,)), dma((T,)),
            dma((spreads,)), dma((T, G)),
        ],
        compiler_params=pltpu.CompilerParams(
            collective_id=0, has_side_effects=True, vmem_limit_bytes=32 * 2**20
        ),
        cost_estimate=pl.CostEstimate(flops=10**9, bytes_accessed=2**23, transcendentals=0),
    )(w, solutions.reshape(inputs, height, width))
    size = PANELS * width
    anywhere = pl.BlockSpec(memory_space=pl.ANY)
    moments, gram_real, gram_imag = pl.pallas_call(
        functools.partial(expand, T),
        out_shape=(
            jax.ShapeDtypeStruct((OUTS, rows, width), bf),
            jax.ShapeDtypeStruct((size, size), jnp.float32),
            jax.ShapeDtypeStruct((size, size), jnp.float32),
        ),
        in_specs=[vmem, vmem],
        out_specs=(anywhere, anywhere, anywhere),
        scratch_shapes=[
            pltpu.VMEM((PANELS, width, size), jnp.float32),
            pltpu.VMEM((PANELS, width, size), jnp.float32),
            dma((2, PANELS)),
            dma,
        ],
        compiler_params=pltpu.CompilerParams(vmem_limit_bytes=32 * 2**20),
        cost_estimate=pl.CostEstimate(flops=10**7, bytes_accessed=2**24, transcendentals=0),
    )(moments, parts_of_gram)
    return moments.reshape(2, PANELS, rows, width), gram_real, gram_imag


def solution(mesh):
    return jax.shard_map(
        functools.partial(local, mesh.shape["shift"], mesh.shape["row"]),
        mesh=mesh,
        in_specs=(P("shift", None, "row", None),),
        out_specs=(P(None, None, ("row", "shift"), None), P(), P()),
        check_vma=False,
    )
```

time: 76.2 us -> 74 us (0.971)
  Pallas kernels: 73.1 us -> 70.9 us
    pallas_call x1, Pallas kernels: 69.4 us -> 67.2 us  [local(): pl.pallas_call(functools.partial(exchange, N, R, rows, part, T, factor),...]
where the time goes in v1:
time: 74 us; the launch traced here: 73.4 us
  Pallas kernels  70.9 us (96%)
  local copies, waits for them, and re-layouts  1.9 us (3%)
    pallas_call x1, Pallas kernels, local(): pl.pallas_call(functools.partial(exchange, N, R, rows, part, T, factor),...  67.2 us
    pallas_call x1, Pallas kernels, local(): pl.pallas_call(functools.partial(expand, T), out_shape=(jax.ShapeDtypeStr...  3.7 us
    unnamed x4, local copies, waits for them, and re-layouts  1.9 us

profile of v1, /device:TPU:0, one launch (start us, length us, event | category | flops | bytes accessed | tf_op | source)
XLA Modules:
  0.0 73.4 jit_solution(1921856833476896879)
XLA Ops:
  0.6 0.0 copy-start
  0.6 1.2 %copy-done = bf16[2,2,1024,128]{3,2,1,0:T(8,128)(2,1)S(1)} copy-done((bf16[2,2,1024,128]{3,2,1,0:T(8,128)(2,1)S(1)}, bf16[2,2,1024,128]{3,2,1,0:T(8,128)(2,1)}, u32[]{:S(2)}) %copy-start) | copy-done | bytes 1048600
  1.9 0.0 copy-start.1
  1.9 0.7 copy-done.1
  2.5 67.2 %shard_map.49 = (bf16[16,64,128]{2,1,0:T(8,128)(2,1)S(1)}, bf16[8,9,64,256]{3,2,1,0:T(8,128)(2,1)S(1)}) custom-call(f32[1024]{0:T(1024)S(1)} %copy-done.1, bf16[4,1024,128]{2,1,0:T(8,128)(2,1)S(1)} %bitcast.2), custom_call_target="tpu_custom_call" | custom-call | flops 1000000000 | bytes 8388608 | tf_op jit(solution)/shard_map/pallas_call | solution.py:421
  69.7 3.7 %shard_map.50 = (bf16[16,64,128]{2,1,0:T(8,128)(2,1)}, f32[1024,1024]{1,0:T(8,128)}, f32[1024,1024]{1,0:T(8,128)}) custom-call(bf16[16,64,128]{2,1,0:T(8,128)(2,1)S(1)} %get-tuple-element.8.m_in, bf16[8,9,64,256]{3,2,1,0:T(8,128)(2,1)S(1)} %get-tuple-element.9.ag_ref), custom_call_target="tpu_custom_call" | custom-call | flops 10000000 | bytes 16777216 | tf_op jit(solution)/shard_map/pallas_call | solution.py:449
Async XLA Ops:
  0.6 1.2 %copy-start = (bf16[2,2,1024,128]{3,2,1,0:T(8,128)(2,1)S(1)}, bf16[2,2,1024,128]{3,2,1,0:T(8,128)(2,1)}, u32[]{:S(2)}) copy-start(bf16[2,2,1024,128]{3,2,1,0:T(8,128)(2,1)} %param.2) | copy-start | bytes 3145732
  1.9 0.7 copy-start.1

commit v2 on v1

--- a/solution.py
+++ b/solution.py
@@ -443,7 +443,7 @@
             collective_id=0, has_side_effects=True, vmem_limit_bytes=32 * 2**20
         ),
         cost_estimate=pl.CostEstimate(flops=10**9, bytes_accessed=2**23, transcendentals=0),
-    )(w, solutions.reshape(inputs, height, width))
+    )(pltpu.with_memory_space_constraint(w, pltpu.HBM), pltpu.with_memory_space_constraint(solutions.reshape(inputs, height, width), pltpu.HBM))
     size = PANELS * width
     anywhere = pl.BlockSpec(memory_space=pl.ANY)
     moments, gram_real, gram_imag = pl.pallas_call(

time: 74 us -> 72 us (0.973)
  local copies, waits for them, and re-layouts: 1.9 us -> 0 us
    unnamed x4 -> x0, local copies, waits for them, and re-layouts: 1.9 us -> none
where the time goes in v2:
time: 72 us; the launch traced here: 71.5 us
  Pallas kernels  70.9 us (98%)
    pallas_call x1, Pallas kernels, local(): pl.pallas_call(functools.partial(exchange, N, R, rows, part, T, factor),...  67.2 us
    pallas_call x1, Pallas kernels, local(): pl.pallas_call(functools.partial(expand, T), out_shape=(jax.ShapeDtypeStr...  3.7 us

profile of v2, /device:TPU:0, one launch (start us, length us, event | category | flops | bytes accessed | tf_op | source)
XLA Modules:
  0.0 71.5 jit_solution(17258251053464195653)
XLA Ops:
  0.6 67.2 %shard_map.49 = (bf16[16,64,128]{2,1,0:T(8,128)(2,1)S(1)}, bf16[8,9,64,256]{3,2,1,0:T(8,128)(2,1)S(1)}) custom-call(f32[1024]{0:T(1024)} %constant.2.clone.w_hbm, bf16[4,1024,128]{2,1,0:T(8,128)(2,1)} %bitcast.2), custom_call_target="tpu_custom_call" | custom-call | flops 1000000000 | bytes 8388608 | tf_op jit(solution)/shard_map/pallas_call | solution.py:421
  67.8 3.7 %shard_map.50 = (bf16[16,64,128]{2,1,0:T(8,128)(2,1)}, f32[1024,1024]{1,0:T(8,128)}, f32[1024,1024]{1,0:T(8,128)}) custom-call(bf16[16,64,128]{2,1,0:T(8,128)(2,1)S(1)} %get-tuple-element.8.m_in, bf16[8,9,64,256]{3,2,1,0:T(8,128)(2,1)S(1)} %get-tuple-element.9.ag_ref), custom_call_target="tpu_custom_call" | custom-call | flops 10000000 | bytes 16777216 | tf_op jit(solution)/shard_map/pallas_call | solution.py:449

commit v3 on v2

v3 whole, which is shorter than its diff:
```python
import functools
import math

import jax
import jax.numpy as jnp
import numpy as np
from jax import lax
from jax.experimental import pallas as pl
from jax.experimental.pallas import tpu as pltpu
from jax.sharding import PartitionSpec as P

PANELS = 8
UNITS = PANELS * PANELS
OUTS = 2 * PANELS
RELAY_LAG = 4
DIAGONAL_LAG = 7
MESH = pl.DeviceIdType.MESH


def coefficients(all_shifts, owners):
    indices = np.arange(all_shifts, dtype=np.float32)
    orders = np.arange(1, PANELS + 1, dtype=np.float32)
    step = (np.float32(2.0 * math.pi) * (indices + np.float32(0.5)) / np.float32(all_shifts)).astype(np.float32)
    angles = (orders[:, None] * step[None, :]).astype(np.float32).astype(np.float64)
    cos_part = np.cos(angles).astype(np.float32) / np.float32(all_shifts)
    sin_part = np.sin(angles).astype(np.float32) / np.float32(all_shifts)
    real_row = np.stack([cos_part, -sin_part], axis=-1)
    imag_row = np.stack([sin_part, cos_part], axis=-1)
    both = np.stack([real_row, imag_row], axis=0).reshape(OUTS, owners, -1)
    return both.transpose(1, 0, 2).reshape(-1).astype(jnp.bfloat16).astype(np.float32)


def unit_place(n):
    k = n // PANELS
    kind = lax.rem(n, PANELS)
    left = jnp.where(kind == 0, k // 2, k)
    apart = jnp.where(kind == 0, PANELS // 2, jnp.where(kind == 1, 0, kind // 2))
    half = jnp.where(kind == 0, lax.rem(k, 2), lax.rem(kind, 2))
    return kind, left, lax.rem(left + apart, PANELS), half


def on_or_above(width):
    i = lax.broadcasted_iota(jnp.int32, (width, width), 0)
    j = lax.broadcasted_iota(jnp.int32, (width, width), 1)
    return i, j


def exchange(
    N, R, rows, part, T, factor,
    w_hbm, x_hbm, m_ref, ag,
    w_ref, x_ref, xs, sbuf, own, dout, din, fo, up, fm,
    in_sems, a2a_s, a2a_r, sg_s, sg_x, sg_r, dd_s, dd_r, up_s, fo_r, out_s, in_r, ag_s, near_r, far_r, rest_r,
):
    Z = N // 4
    CH = rows // part
    s = lax.axis_index("shift")
    r = lax.axis_index("row")
    core = lax.rem(s, 2)
    z = s // 4
    x = lax.rem(s // 2, 2)
    inputs = x_ref.shape[0]
    width = x_ref.shape[2]
    cut = width // 2
    slots = 2 * R
    G = 4 * R

    def member(x_, r_, c_):
        return (r_ * 2 + x_) * 2 + c_

    def place(z_, x_, c_):
        return (z_ * 2 + x_) * 2 + c_

    p = member(x, r, core)
    here = r * 2 + x
    partner = place(z, x, 1 - core)
    across = place(z, 1 - x, core)

    def row_at(i):
        return lax.rem(r + i + R, R)

    def remote(src, dst, ss, rr, to_s, to_r):
        return pltpu.make_async_remote_copy(
            src_ref=src, dst_ref=dst, send_sem=ss, recv_sem=rr,
            device_id={"shift": to_s, "row": to_r}, device_id_type=MESH,
        )

    def arrived(ref, sem):
        remote(ref, ref, a2a_s, sem, s, r).wait_recv()

    def left(ref, sem):
        remote(ref, ref, sem, rest_r, s, r).wait_send()

    load_x = pltpu.make_async_copy(x_hbm, x_ref, in_sems.at[0])
    load_w = pltpu.make_async_copy(w_hbm, w_ref, in_sems.at[1])
    load_x.start()
    load_w.start()
    barrier = pltpu.get_barrier_semaphore()
    for i in range(1, N):
        pl.semaphore_signal(barrier, inc=1, device_id={"shift": lax.rem(s + i, N), "row": r}, device_id_type=MESH)
    for i in range(1, R):
        for to in (s, across):
            pl.semaphore_signal(barrier, inc=1, device_id={"shift": to, "row": row_at(i)}, device_id_type=MESH)
    load_x.wait()
    load_w.wait()
    pl.semaphore_wait(barrier, N - 1 + 2 * (R - 1))


    def rows_of(owner, h):
        return pl.ds(pl.multiple_of(owner * rows + h * part, part), part)

    def send_rows(h, to):
        slot = lax.rem(to - s + N, N) - 1
        remote(x_ref.at[:, rows_of(to, h), :], xs.at[h, slot], a2a_s, a2a_r.at[h], to, r).start()

    def send_chunk(h, c):
        for e in range(Z // 2):
            for to_z in (e, Z - 1 - e):
                for dx, dc in ((0, 0), (1, 0), (0, 1), (1, 1)):
                    to = place(to_z, lax.rem(x + dx, 2), lax.rem(core + dc, 2))
                    if dx or dc:
                        send_rows(h, to)
                    else:
                        @pl.when(to_z != z)
                        def _():
                            send_rows(h, to)
        return c

    lax.fori_loop(0, CH, send_chunk, 0)


    def weigh(acc, blocks, source):
        parts = [b.astype(jnp.float32) for b in blocks]
        out = []
        for o in range(OUTS):
            base = (source * OUTS + o) * inputs
            total = parts[0] * w_ref[base]
            for c in range(1, inputs):
                total += parts[c] * w_ref[base + c]
            out.append(total if acc is None else acc[o] + total)
        return tuple(out)

    def panels_to(h, slot, sem, to_s, to_r):
        remote(sbuf.at[h, slot], sbuf.at[h, slot], sg_s, sem, to_s, to_r).start()

    def moments_of(h, c):
        acc = weigh(None, [x_ref[q, rows_of(s, h), :] for q in range(inputs)], s)
        arrived(xs.at[h], a2a_r.at[h])

        def take(j, acc):
            return weigh(acc, [xs[h, j, q] for q in range(inputs)], lax.rem(s - 1 - j + N, N))

        acc = lax.fori_loop(0, N - 1, take, acc)
        at = pl.ds(pl.multiple_of(h * part, part), part)
        for o in range(OUTS):
            value = acc[o].astype(jnp.bfloat16)
            sbuf[h, here, o] = value
            m_ref[o, at, :] = value
        panels_to(h, here, sg_x.at[h], across, r)
        for i in range(1, R):
            panels_to(h, here, sg_r, s, row_at(i))
        return c

    def relay_panels(h):
        slot = r * 2 + 1 - x
        arrived(sbuf.at[h, slot], sg_x.at[h])
        for i in range(1, R):
            panels_to(h, slot, sg_r, s, row_at(i))

    def moments_and_relay(h, c):
        moments_of(h, c)
        relay_panels(h)
        return c

    lax.fori_loop(0, CH - 1, moments_and_relay, 0)
    moments_of(CH - 1, 0)
    for i in range(1, R):
        panels_to(CH - 1, here, sg_r, across, row_at(i))
    arrived(sbuf.at[CH - 1, 0], sg_x.at[CH - 1])
    arrived(sbuf.at[:, pl.ds(0, slots - 2)], sg_r)


    depth = slots * rows
    dims = (((0,), (0,)), ((), ()))

    def panel(k):
        return jnp.concatenate(
            [sbuf[:, :, k].reshape(depth, width), sbuf[:, :, PANELS + k].reshape(depth, width)], axis=1
        )

    def product(a, b):
        v = lax.dot_general(a, b, dims, preferred_element_type=jnp.float32) * factor
        return v[:width, :width] + v[width:, width:], v[:width, width:] - v[width:, :width]

    def halves(re, im):
        return [jnp.concatenate([re[h], im[h]], axis=1) for h in (slice(0, cut), slice(cut, width))]

    def packed(re, im):
        i, j = on_or_above(width)
        v = jnp.where(i <= j, re, im)
        return jnp.concatenate([v[:cut], v[cut:]], axis=1)

    def swap(t):
        return remote(dout.at[t], din.at[t], dd_s, dd_r.at[t], partner, r)

    def give(t, value):
        dout[t] = value.astype(jnp.bfloat16)
        swap(t).start()

    other = member(x, r, 1 - core)
    if T == PANELS:
        low, high = halves(*product(panel(here), panel(here + PANELS // 2)))
        give(0, jnp.where(core == 0, high, low))
        own[0] = jnp.where(core == 0, low, high)
        a = panel(other)
        give(1, packed(*product(a, a)))
        for d in range(1, PANELS // 2):
            low, high = halves(*product(a, panel(lax.rem(other + d, PANELS))))
            give(2 * d, low)
            give(2 * d + 1, high)
        a = panel(p)
        own[1] = packed(*product(a, a))
        for d in range(1, PANELS // 2):
            own[2 * d], own[2 * d + 1] = halves(*product(a, panel(lax.rem(p + d, PANELS))))
    else:
        def unit(n):
            kind, k, q, half = unit_place(n)
            re, im = product(panel(k), panel(q))
            low, high = halves(re, im)
            return jnp.where(kind == 1, packed(re, im), jnp.where(half == 0, low, high))

        def theirs(t, c):
            give(t, unit(other * T + t))
            return c

        def mine(t, c):
            own[t] = unit(p * T + t)
            return c

        lax.fori_loop(0, T, theirs, 0)
        lax.fori_loop(0, T, mine, 0)


    lower = z < Z // 2
    inner = jnp.where(lower, z + 1, z - 1)
    outer = jnp.where(lower, z - 1, z + 1)
    from_end = jnp.where(lower, z, Z - 1 - z)
    is_middle = from_end == Z // 2 - 1
    has_outer = from_end > 0
    inner_s = place(inner, x, core)
    outer_s = place(jnp.where(has_outer, outer, inner), x, core)

    def climb(t, c):
        arrived(din.at[t], dd_r.at[t])
        own[t] = own[t] + din[t].astype(jnp.float32)

        @pl.when(has_outer)
        def _():
            arrived(fo.at[t], fo_r.at[t])
            own[t] = own[t] + fo[t].astype(jnp.float32)

        up[t] = own[t].astype(jnp.bfloat16)

        @pl.when(is_middle)
        def _():
            remote(up.at[t], fm.at[t], up_s, in_r.at[t], inner_s, r).start()

        @pl.when(jnp.logical_not(is_middle))
        def _():
            remote(up.at[t], fo.at[t], up_s, fo_r.at[t], inner_s, r).start()

        return c

    lax.fori_loop(0, T, climb, 0)


    def forward(t, slot, sem, to_s, to_r):
        remote(ag.at[slot, t], ag.at[slot, t], ag_s, sem, to_s, to_r).start()

    def total(t):
        @pl.when(is_middle)
        def _():
            arrived(fm.at[t], in_r.at[t])
            ag[p, t] = (up[t].astype(jnp.float32) + fm[t].astype(jnp.float32)).astype(jnp.bfloat16)

        @pl.when(jnp.logical_not(is_middle))
        def _():
            arrived(ag.at[p, t], in_r.at[t])

        @pl.when(has_outer)
        def _():
            remote(ag.at[p, t], ag.at[p, t], out_s, in_r.at[t], outer_s, r).start()

    def spread(t):
        forward(t, p, near_r.at[t], across, r)
        for i in range(1, R):
            forward(t, p, near_r.at[t], s, row_at(i))
        forward(t, p, rest_r, partner, r)

    def relay(t):
        arrived(ag.at[pl.ds(0, R), t], near_r.at[t])
        first = core == 0
        for i in range(1, R):
            slot = jnp.where(first, member(1 - x, r, core), member(x, row_at(-i), core))
            forward(t, slot, far_r.at[t], jnp.where(first, s, across), jnp.where(first, row_at(i), r))
        forward(t, member(1 - x, r, core), rest_r, partner, r)
        for i in range(1, R):
            forward(t, member(x, row_at(-i), core), rest_r, partner, r)

    def diagonal(t):
        arrived(ag.at[pl.ds(0, R - 1), t], far_r.at[t])
        for i in range(1, R):
            forward(t, member(1 - x, row_at(-i), core), rest_r, partner, r)

    for n in range(T + DIAGONAL_LAG):
        if n < T:
            total(n)
            spread(n)
        if 0 <= n - RELAY_LAG < T:
            relay(n - RELAY_LAG)
        if 0 <= n - DIAGONAL_LAG < T:
            diagonal(n - DIAGONAL_LAG)
    arrived(ag.at[pl.ds(0, slots)], rest_r)


    left(xs, a2a_s)
    left(sbuf.at[:, pl.ds(0, slots - 1)], sg_s)
    left(dout, dd_s)
    left(up, up_s)

    @pl.when(has_outer)
    def _():
        left(up, out_s)

    left(ag.at[pl.ds(0, G - 1)], ag_s)


def expand(T, m_in, ag_ref, m_out, re_out, im_out, re_buf, im_buf, sems, m_sem):
    width = re_buf.shape[1]
    half = PANELS // 2
    keep = pltpu.make_async_copy(m_in, m_out, m_sem)
    keep.start()

    def unit(n):
        return ag_ref[n // T, lax.rem(n, T)].astype(jnp.float32)

    def pair(k, d):
        v = jnp.concatenate([unit(PANELS * k + 2 * d), unit(PANELS * k + 2 * d + 1)], axis=0)
        return v[:, :width], v[:, width:]

    def writes(k, slot):
        at = pl.ds(pl.multiple_of(k * width, width), width)
        return (
            pltpu.make_async_copy(re_buf.at[k], re_out.at[at], sems.at[0, k]),
            pltpu.make_async_copy(im_buf.at[k], im_out.at[at], sems.at[1, k]),
        )

    def one(k, c):
        for d in range(PANELS):
            q = lax.rem(k + d, PANELS)
            at = pl.ds(pl.multiple_of(q * width, width), width)
            if d == 0:
                v = unit(PANELS * k + 1)
                v = jnp.concatenate([v[:, :width], v[:, width:]], axis=0)
                i, j = on_or_above(width)
                re = jnp.where(i <= j, v, v.T)
                im = jnp.where(i > j, v, jnp.where(i < j, -v.T, 0.0))
            elif d < half:
                re, im = pair(k, d)
            elif d == half:
                first = jnp.minimum(k, q)
                v = jnp.concatenate([unit(2 * PANELS * first), unit(2 * PANELS * first + PANELS)], axis=0)
                re, im = v[:, :width], v[:, width:]
                re, im = jnp.where(k < half, re, re.T), jnp.where(k < half, im, -im.T)
            else:
                re, im = pair(q, PANELS - d)
                re, im = re.T, -im.T
            re_buf[k, :, at] = re
            im_buf[k, :, at] = im
        for copy in writes(k, k):
            copy.start()
        return c

    lax.fori_loop(0, PANELS, one, 0)

    def finish(k, c):
        for copy in writes(k, k):
            copy.wait()
        return c

    lax.fori_loop(0, PANELS, finish, 0)
    keep.wait()


def local(N, R, solutions):
    shifts, parts, height, width = solutions.shape
    rows = height // N
    G = 4 * R
    T = UNITS // G
    assert T * G == UNITS
    cut = width // 2
    inputs = shifts * parts
    part = 16 if rows % 16 == 0 else rows
    chunks = rows // part
    factor = 1.0 / math.sqrt(height * R)
    w = jnp.asarray(coefficients(shifts * N, N))
    bf, dma = jnp.bfloat16, pltpu.SemaphoreType.DMA
    vmem = pl.BlockSpec(memory_space=pltpu.VMEM)
    hbm = pl.BlockSpec(memory_space=pltpu.HBM)
    unit = (T, cut, 2 * width)
    moments, parts_of_gram = pl.pallas_call(
        functools.partial(exchange, N, R, rows, part, T, factor),
        out_shape=(
            jax.ShapeDtypeStruct((OUTS, rows, width), bf),
            jax.ShapeDtypeStruct((G,) + unit, bf),
        ),
        in_specs=[hbm, hbm],
        out_specs=(vmem, vmem),
        scratch_shapes=[
            pltpu.SMEM(w.shape, jnp.float32),
            pltpu.VMEM((inputs, height, width), bf),
            pltpu.VMEM((chunks, N - 1, inputs, part, width), bf),
            pltpu.VMEM((chunks, 2 * R, OUTS, part, width), bf),
            pltpu.VMEM(unit, jnp.float32),
            pltpu.VMEM(unit, bf), pltpu.VMEM(unit, bf), pltpu.VMEM(unit, bf),
            pltpu.VMEM(unit, bf), pltpu.VMEM(unit, bf),
            dma((2,)),
            dma, dma((chunks,)), dma, dma((chunks,)), dma,
            dma, dma((T,)), dma, dma((T,)), dma, dma((T,)),
            dma, dma((T,)), dma((T,)), dma,
        ],
        compiler_params=pltpu.CompilerParams(
            collective_id=0, has_side_effects=True, vmem_limit_bytes=32 * 2**20
        ),
        cost_estimate=pl.CostEstimate(flops=10**9, bytes_accessed=2**23, transcendentals=0),
    )(
        pltpu.with_memory_space_constraint(w, pltpu.HBM),
        pltpu.with_memory_space_constraint(solutions.reshape(inputs, height, width), pltpu.HBM),
    )
    size = PANELS * width
    anywhere = pl.BlockSpec(memory_space=pl.ANY)
    moments, gram_real, gram_imag = pl.pallas_call(
        functools.partial(expand, T),
        out_shape=(
            jax.ShapeDtypeStruct((OUTS, rows, width), bf),
            jax.ShapeDtypeStruct((size, size), jnp.float32),
            jax.ShapeDtypeStruct((size, size), jnp.float32),
        ),
        in_specs=[vmem, vmem],
        out_specs=(anywhere, anywhere, anywhere),
        scratch_shapes=[
            pltpu.VMEM((PANELS, width, size), jnp.float32),
            pltpu.VMEM((PANELS, width, size), jnp.float32),
            dma((2, PANELS)),
            dma,
        ],
        compiler_params=pltpu.CompilerParams(vmem_limit_bytes=32 * 2**20),
        cost_estimate=pl.CostEstimate(flops=10**7, bytes_accessed=2**24, transcendentals=0),
    )(moments, parts_of_gram)
    return moments.reshape(2, PANELS, rows, width), gram_real, gram_imag


def solution(mesh):
    return jax.shard_map(
        functools.partial(local, mesh.shape["shift"], mesh.shape["row"]),
        mesh=mesh,
        in_specs=(P("shift", None, "row", None),),
        out_specs=(P(None, None, ("row", "shift"), None), P(), P()),
        check_vma=False,
    )
```

time: 72 us -> 66.5 us (0.924)
  Pallas kernels: 70.9 us -> 65.7 us
    pallas_call x1, Pallas kernels: 67.2 us -> 62.1 us  [local(): pl.pallas_call(functools.partial(exchange, N, R, rows, part, T, factor),...]
where the time goes in v3:
time: 66.5 us; the launch traced here: 66.4 us
  Pallas kernels  65.7 us (99%)
    pallas_call x1, Pallas kernels, local(): pl.pallas_call(functools.partial(exchange, N, R, rows, part, T, factor),...  62.1 us
    pallas_call x1, Pallas kernels, local(): pl.pallas_call(functools.partial(expand, T), out_shape=(jax.ShapeDtypeStr...  3.69 us

profile of v3, /device:TPU:0, one launch (start us, length us, event | category | flops | bytes accessed | tf_op | source)
XLA Modules:
  0.0 66.4 jit_solution(12489605800213035181)
XLA Ops:
  0.6 62.1 %shard_map.49 = (bf16[16,64,128]{2,1,0:T(8,128)(2,1)S(1)}, bf16[8,8,64,256]{3,2,1,0:T(8,128)(2,1)S(1)}) custom-call(f32[1024]{0:T(1024)} %constant.2.clone.w_hbm, bf16[4,1024,128]{2,1,0:T(8,128)(2,1)} %bitcast.2), custom_call_target="tpu_custom_call" | custom-call | flops 1000000000 | bytes 8388608 | tf_op jit(solution)/shard_map/pallas_call | solution.py:410
  62.7 3.7 %shard_map.50 = (bf16[16,64,128]{2,1,0:T(8,128)(2,1)}, f32[1024,1024]{1,0:T(8,128)}, f32[1024,1024]{1,0:T(8,128)}) custom-call(bf16[16,64,128]{2,1,0:T(8,128)(2,1)S(1)} %get-tuple-element.8.m_in, bf16[8,8,64,256]{3,2,1,0:T(8,128)(2,1)S(1)} %get-tuple-element.9.ag_ref), custom_call_target="tpu_custom_call" | custom-call | flops 10000000 | bytes 16777216 | tf_op jit(solution)/shard_map/pallas_call | solution.py:441

commit v4 on v3

--- a/solution.py
+++ b/solution.py
@@ -12,6 +12,11 @@
 PANELS = 8
 UNITS = PANELS * PANELS
 OUTS = 2 * PANELS
+CHUNK_ROWS = 16
+LEAD = 2
+DIRECT = 2
+CLOSE_UNITS = 2
+SWAP_LAG = 4
 RELAY_LAG = 4
 DIAGONAL_LAG = 7
 MESH = pl.DeviceIdType.MESH
@@ -49,7 +54,7 @@
     N, R, rows, part, T, factor,
     w_hbm, x_hbm, m_ref, ag,
     w_ref, x_ref, xs, sbuf, own, dout, din, fo, up, fm,
-    in_sems, a2a_s, a2a_r, sg_s, sg_x, sg_r, dd_s, dd_r, up_s, fo_r, out_s, in_r, ag_s, near_r, far_r, rest_r,
+    in_sems, a2a_s, a2a_r, sg_s, sg_x, sg_r, sg_last, dd_s, dd_r, up_s, fo_r, out_s, in_r, ag_s, near_r, far_r, rest_r,
 ):
     Z = N // 4
     CH = rows // part
@@ -125,7 +130,7 @@
                             send_rows(h, to)
         return c
 
-    lax.fori_loop(0, CH, send_chunk, 0)
+    lax.fori_loop(0, min(LEAD, CH), send_chunk, 0)
 
 
     def weigh(acc, blocks, source):
@@ -142,9 +147,13 @@
     def panels_to(h, slot, sem, to_s, to_r):
         remote(sbuf.at[h, slot], sbuf.at[h, slot], sg_s, sem, to_s, to_r).start()
 
-    def moments_of(h, c):
+    def moments_of(h, c, direct):
         acc = weigh(None, [x_ref[q, rows_of(s, h), :] for q in range(inputs)], s)
         arrived(xs.at[h], a2a_r.at[h])
+
+        @pl.when(h + LEAD < CH)
+        def _():
+            send_chunk(h + LEAD, 0)
 
         def take(j, acc):
             return weigh(acc, [xs[h, j, q] for q in range(inputs)], lax.rem(s - 1 - j + N, N))
@@ -155,10 +164,12 @@
             value = acc[o].astype(jnp.bfloat16)
             sbuf[h, here, o] = value
             m_ref[o, at, :] = value
-        panels_to(h, here, sg_x.at[h], across, r)
+        if direct:
+            for i in range(1, R):
+                panels_to(h, here, sg_r, across, row_at(i))
+        panels_to(h, here, sg_last if direct else sg_x.at[h], across, r)
         for i in range(1, R):
             panels_to(h, here, sg_r, s, row_at(i))
-        return c
 
     def relay_panels(h):
         slot = r * 2 + 1 - x
@@ -167,15 +178,19 @@
             panels_to(h, slot, sg_r, s, row_at(i))
 
     def moments_and_relay(h, c):
-        moments_of(h, c)
+        moments_of(h, c, False)
         relay_panels(h)
         return c
 
-    lax.fori_loop(0, CH - 1, moments_and_relay, 0)
-    moments_of(CH - 1, 0)
-    for i in range(1, R):
-        panels_to(CH - 1, here, sg_r, across, row_at(i))
-    arrived(sbuf.at[CH - 1, 0], sg_x.at[CH - 1])
+    last = max(CH - DIRECT, 0)
+    lax.fori_loop(0, last, moments_and_relay, 0)
+
+    def moments_direct(h, c):
+        moments_of(h, c, True)
+        return c
+
+    lax.fori_loop(last, CH, moments_direct, 0)
+    arrived(sbuf.at[pl.ds(last, CH - last), 0], sg_last)
     arrived(sbuf.at[:, pl.ds(0, slots - 2)], sg_r)
 
 
@@ -188,7 +203,7 @@
         )
 
     def product(a, b):
-        v = lax.dot_general(a, b, dims, preferred_element_type=jnp.float32) * factor
+        v = lax.dot_general(a, b, dims, preferred_element_type=jnp.float32)
         return v[:width, :width] + v[width:, width:], v[:width, width:] - v[width:, :width]
 
     def halves(re, im):
@@ -205,6 +220,78 @@
     def give(t, value):
         dout[t] = value.astype(jnp.bfloat16)
         swap(t).start()
+
+
+    lower = z < Z // 2
+    inner = jnp.where(lower, z + 1, z - 1)
+    outer = jnp.where(lower, z - 1, z + 1)
+    from_end = jnp.where(lower, z, Z - 1 - z)
+    is_middle = from_end == Z // 2 - 1
+    has_outer = from_end > 0
+    inner_s = place(inner, x, core)
+    outer_s = place(jnp.where(has_outer, outer, inner), x, core)
+
+    def climb(t, c):
+        arrived(din.at[t], dd_r.at[t])
+        own[t] = (own[t] + din[t].astype(jnp.float32)) * factor
+
+        @pl.when(has_outer)
+        def _():
+            arrived(fo.at[t], fo_r.at[t])
+            own[t] = own[t] + fo[t].astype(jnp.float32)
+
+        up[t] = own[t].astype(jnp.bfloat16)
+
+        @pl.when(is_middle)
+        def _():
+            remote(up.at[t], fm.at[t], up_s, in_r.at[t], inner_s, r).start()
+
+        @pl.when(jnp.logical_not(is_middle))
+        def _():
+            remote(up.at[t], fo.at[t], up_s, fo_r.at[t], inner_s, r).start()
+
+        return c
+
+
+    def forward(t, slot, sem, to_s, to_r):
+        remote(ag.at[slot, t], ag.at[slot, t], ag_s, sem, to_s, to_r).start()
+
+    def total(t):
+        @pl.when(is_middle)
+        def _():
+            arrived(fm.at[t], in_r.at[t])
+            ag[p, t] = (up[t].astype(jnp.float32) + fm[t].astype(jnp.float32)).astype(jnp.bfloat16)
+
+        @pl.when(jnp.logical_not(is_middle))
+        def _():
+            arrived(ag.at[p, t], in_r.at[t])
+
+        @pl.when(has_outer)
+        def _():
+            remote(ag.at[p, t], ag.at[p, t], out_s, in_r.at[t], outer_s, r).start()
+
+    def close(t):
+        return t >= T - CLOSE_UNITS
+
+    def spread(t):
+        if close(t):
+            for i in range(1, R):
+                forward(t, p, far_r.at[t], across, row_at(i))
+        forward(t, p, near_r.at[t], across, r)
+        for i in range(1, R):
+            forward(t, p, near_r.at[t], s, row_at(i))
+        forward(t, p, rest_r, partner, r)
+
+    def finish(t):
+        total(t)
+        spread(t)
+
+    def climb_and_finish(t):
+        climb(t, 0)
+        if t >= SWAP_LAG:
+            @pl.when(is_middle)
+            def _():
+                finish(t - SWAP_LAG)
 
     other = member(x, r, 1 - core)
     if T == PANELS:
@@ -217,10 +304,14 @@
             low, high = halves(*product(a, panel(lax.rem(other + d, PANELS))))
             give(2 * d, low)
             give(2 * d + 1, high)
+        climb_and_finish(0)
         a = panel(p)
         own[1] = packed(*product(a, a))
+        climb_and_finish(1)
         for d in range(1, PANELS // 2):
             own[2 * d], own[2 * d + 1] = halves(*product(a, panel(lax.rem(p + d, PANELS))))
+            climb_and_finish(2 * d)
+            climb_and_finish(2 * d + 1)
     else:
         def unit(n):
             kind, k, q, half = unit_place(n)
@@ -238,68 +329,13 @@
 
         lax.fori_loop(0, T, theirs, 0)
         lax.fori_loop(0, T, mine, 0)
-
-
-    lower = z < Z // 2
-    inner = jnp.where(lower, z + 1, z - 1)
-    outer = jnp.where(lower, z - 1, z + 1)
-    from_end = jnp.where(lower, z, Z - 1 - z)
-    is_middle = from_end == Z // 2 - 1
-    has_outer = from_end > 0
-    inner_s = place(inner, x, core)
-    outer_s = place(jnp.where(has_outer, outer, inner), x, core)
-
-    def climb(t, c):
-        arrived(din.at[t], dd_r.at[t])
-        own[t] = own[t] + din[t].astype(jnp.float32)
-
-        @pl.when(has_outer)
-        def _():
-            arrived(fo.at[t], fo_r.at[t])
-            own[t] = own[t] + fo[t].astype(jnp.float32)
-
-        up[t] = own[t].astype(jnp.bfloat16)
-
-        @pl.when(is_middle)
-        def _():
-            remote(up.at[t], fm.at[t], up_s, in_r.at[t], inner_s, r).start()
-
-        @pl.when(jnp.logical_not(is_middle))
-        def _():
-            remote(up.at[t], fo.at[t], up_s, fo_r.at[t], inner_s, r).start()
-
-        return c
-
-    lax.fori_loop(0, T, climb, 0)
-
-
-    def forward(t, slot, sem, to_s, to_r):
-        remote(ag.at[slot, t], ag.at[slot, t], ag_s, sem, to_s, to_r).start()
-
-    def total(t):
-        @pl.when(is_middle)
-        def _():
-            arrived(fm.at[t], in_r.at[t])
-            ag[p, t] = (up[t].astype(jnp.float32) + fm[t].astype(jnp.float32)).astype(jnp.bfloat16)
-
-        @pl.when(jnp.logical_not(is_middle))
-        def _():
-            arrived(ag.at[p, t], in_r.at[t])
-
-        @pl.when(has_outer)
-        def _():
-            remote(ag.at[p, t], ag.at[p, t], out_s, in_r.at[t], outer_s, r).start()
-
-    def spread(t):
-        forward(t, p, near_r.at[t], across, r)
-        for i in range(1, R):
-            forward(t, p, near_r.at[t], s, row_at(i))
-        forward(t, p, rest_r, partner, r)
+        for t in range(T):
+            climb_and_finish(t)
 
     def relay(t):
         arrived(ag.at[pl.ds(0, R), t], near_r.at[t])
         first = core == 0
-        for i in range(1, R):
+        for i in range(1, R if not close(t) else 1):
             slot = jnp.where(first, member(1 - x, r, core), member(x, row_at(-i), core))
             forward(t, slot, far_r.at[t], jnp.where(first, s, across), jnp.where(first, row_at(i), r))
         forward(t, member(1 - x, r, core), rest_r, partner, r)
@@ -312,9 +348,12 @@
             forward(t, member(1 - x, row_at(-i), core), rest_r, partner, r)
 
     for n in range(T + DIAGONAL_LAG):
-        if n < T:
-            total(n)
-            spread(n)
+        if n < T - SWAP_LAG:
+            @pl.when(jnp.logical_not(is_middle))
+            def _():
+                finish(n)
+        elif n < T:
+            finish(n)
         if 0 <= n - RELAY_LAG < T:
             relay(n - RELAY_LAG)
         if 0 <= n - DIAGONAL_LAG < T:
@@ -399,7 +438,7 @@
     assert T * G == UNITS
     cut = width // 2
     inputs = shifts * parts
-    part = 16 if rows % 16 == 0 else rows
+    part = CHUNK_ROWS if rows % CHUNK_ROWS == 0 else rows
     chunks = rows // part
     factor = 1.0 / math.sqrt(height * R)
     w = jnp.asarray(coefficients(shifts * N, N))
@@ -424,7 +463,7 @@
             pltpu.VMEM(unit, bf), pltpu.VMEM(unit, bf), pltpu.VMEM(unit, bf),
             pltpu.VMEM(unit, bf), pltpu.VMEM(unit, bf),
             dma((2,)),
-            dma, dma((chunks,)), dma, dma((chunks,)), dma,
+            dma, dma((chunks,)), dma, dma((chunks,)), dma, dma,
             dma, dma((T,)), dma, dma((T,)), dma, dma((T,)),
             dma, dma((T,)), dma((T,)), dma,
         ],

time: 66.5 us -> 63.1 us (0.949)
  Pallas kernels: 65.7 us -> 62.3 us
    pallas_call x1, Pallas kernels: 62.1 us -> 58.6 us  [local(): pl.pallas_call(functools.partial(exchange, N, R, rows, part, T, factor),...]
where the time goes in v4:
time: 63.1 us; the launch traced here: 62.9 us
  Pallas kernels  62.3 us (99%)
  between operations  0.64 us (1%)
    pallas_call x1, Pallas kernels, local(): pl.pallas_call(functools.partial(exchange, N, R, rows, part, T, factor),...  58.6 us
    pallas_call x1, Pallas kernels, local(): pl.pallas_call(functools.partial(expand, T), out_shape=(jax.ShapeDtypeStr...  3.69 us

profile of v4, /device:TPU:0, one launch (start us, length us, event | category | flops | bytes accessed | tf_op | source)
XLA Modules:
  0.0 62.9 jit_solution(10263934762432525605)
XLA Ops:
  0.6 58.6 %shard_map.49 = (bf16[16,64,128]{2,1,0:T(8,128)(2,1)S(1)}, bf16[8,8,64,256]{3,2,1,0:T(8,128)(2,1)S(1)}) custom-call(f32[1024]{0:T(1024)} %constant.2.clone.w_hbm, bf16[4,1024,128]{2,1,0:T(8,128)(2,1)} %bitcast.2), custom_call_target="tpu_custom_call" | custom-call | flops 1000000000 | bytes 8388608 | tf_op jit(solution)/shard_map/pallas_call | solution.py:449
  59.2 3.7 %shard_map.50 = (bf16[16,64,128]{2,1,0:T(8,128)(2,1)}, f32[1024,1024]{1,0:T(8,128)}, f32[1024,1024]{1,0:T(8,128)}) custom-call(bf16[16,64,128]{2,1,0:T(8,128)(2,1)S(1)} %get-tuple-element.8.m_in, bf16[8,8,64,256]{3,2,1,0:T(8,128)(2,1)S(1)} %get-tuple-element.9.ag_ref), custom_call_target="tpu_custom_call" | custom-call | flops 10000000 | bytes 16777216 | tf_op jit(solution)/shard_map/pallas_call | solution.py:480

commit v5 on v4

--- a/solution.py
+++ b/solution.py
@@ -15,10 +15,12 @@
 CHUNK_ROWS = 16
 LEAD = 2
 DIRECT = 2
-CLOSE_UNITS = 2
-SWAP_LAG = 4
-RELAY_LAG = 4
-DIAGONAL_LAG = 7
+PIECES = 2
+CLOSE_PIECES = 4
+SWAP_LAG = 8
+OVER_Z = (1, 2, 3)
+RELAY_LAG = 6
+DIAGONAL_LAG = 11
 MESH = pl.DeviceIdType.MESH
 
 
@@ -54,7 +56,7 @@
     N, R, rows, part, T, factor,
     w_hbm, x_hbm, m_ref, ag,
     w_ref, x_ref, xs, sbuf, own, dout, din, fo, up, fm,
-    in_sems, a2a_s, a2a_r, sg_s, sg_x, sg_r, sg_last, dd_s, dd_r, up_s, fo_r, out_s, in_r, ag_s, near_r, far_r, rest_r,
+    in_sems, a2a_s, a2a_r, sg_s, sg_x, sg_r, sg_last, dd_s, dd_r, up_s, fo_r, out_s, in_r, ag_s, near_r, far_r, rest_r, over_s,
 ):
     Z = N // 4
     CH = rows // part
@@ -66,6 +68,8 @@
     inputs = x_ref.shape[0]
     width = x_ref.shape[2]
     cut = width // 2
+    piece = cut // PIECES
+    U = T * PIECES
     slots = 2 * R
     G = 4 * R
 
@@ -115,7 +119,7 @@
 
     def send_rows(h, to):
         slot = lax.rem(to - s + N, N) - 1
-        remote(x_ref.at[:, rows_of(to, h), :], xs.at[h, slot], a2a_s, a2a_r.at[h], to, r).start()
+        remote(x_ref.at[:, rows_of(to, h), :], xs.at[h, slot], a2a_s, a2a_r.at[h, jnp.where(slot < N // 2, 0, 1)], to, r).start()
 
     def send_chunk(h, c):
         for e in range(Z // 2):
@@ -149,16 +153,19 @@
 
     def moments_of(h, c, direct):
         acc = weigh(None, [x_ref[q, rows_of(s, h), :] for q in range(inputs)], s)
-        arrived(xs.at[h], a2a_r.at[h])
-
-        @pl.when(h + LEAD < CH)
-        def _():
-            send_chunk(h + LEAD, 0)
+        arrived(xs.at[h, pl.ds(0, N // 2)], a2a_r.at[h, 0])
 
         def take(j, acc):
             return weigh(acc, [xs[h, j, q] for q in range(inputs)], lax.rem(s - 1 - j + N, N))
 
-        acc = lax.fori_loop(0, N - 1, take, acc)
+        acc = lax.fori_loop(0, N // 2, take, acc)
+        arrived(xs.at[h, pl.ds(N // 2, N - 1 - N // 2)], a2a_r.at[h, 1])
+
+        @pl.when(h + LEAD < CH)
+        def _():
+            send_chunk(h + LEAD, 0)
+
+        acc = lax.fori_loop(N // 2, N - 1, take, acc)
         at = pl.ds(pl.multiple_of(h * part, part), part)
         for o in range(OUTS):
             value = acc[o].astype(jnp.bfloat16)
@@ -195,15 +202,17 @@
 
 
     depth = slots * rows
-    dims = (((0,), (0,)), ((), ()))
 
     def panel(k):
         return jnp.concatenate(
             [sbuf[:, :, k].reshape(depth, width), sbuf[:, :, PANELS + k].reshape(depth, width)], axis=1
         )
 
+    def turned(k):
+        return panel(k).T
+
     def product(a, b):
-        v = lax.dot_general(a, b, dims, preferred_element_type=jnp.float32)
+        v = jnp.dot(a, b, preferred_element_type=jnp.float32)
         return v[:width, :width] + v[width:, width:], v[:width, width:] - v[width:, :width]
 
     def halves(re, im):
@@ -231,91 +240,95 @@
     inner_s = place(inner, x, core)
     outer_s = place(jnp.where(has_outer, outer, inner), x, core)
 
-    def climb(t, c):
-        arrived(din.at[t], dd_r.at[t])
-        own[t] = (own[t] + din[t].astype(jnp.float32)) * factor
+    def of(u):
+        return u // PIECES, slice(u % PIECES * piece, u % PIECES * piece + piece)
+
+    def climb(u):
+        t, at = of(u)
+        if u % PIECES == 0:
+            arrived(din.at[t], dd_r.at[t])
+        own[t, at] = (own[t, at] + din[t, at].astype(jnp.float32)) * factor
 
         @pl.when(has_outer)
         def _():
-            arrived(fo.at[t], fo_r.at[t])
-            own[t] = own[t] + fo[t].astype(jnp.float32)
-
-        up[t] = own[t].astype(jnp.bfloat16)
+            arrived(fo.at[t, at], fo_r.at[u])
+            own[t, at] = own[t, at] + fo[t, at].astype(jnp.float32)
+
+        up[t, at] = own[t, at].astype(jnp.bfloat16)
 
         @pl.when(is_middle)
         def _():
-            remote(up.at[t], fm.at[t], up_s, in_r.at[t], inner_s, r).start()
+            remote(up.at[t, at], fm.at[t, at], up_s, in_r.at[u], inner_s, r).start()
 
         @pl.when(jnp.logical_not(is_middle))
         def _():
-            remote(up.at[t], fo.at[t], up_s, fo_r.at[t], inner_s, r).start()
-
-        return c
-
-
-    def forward(t, slot, sem, to_s, to_r):
-        remote(ag.at[slot, t], ag.at[slot, t], ag_s, sem, to_s, to_r).start()
-
-    def total(t):
+            remote(up.at[t, at], fo.at[t, at], up_s, fo_r.at[u], inner_s, r).start()
+
+    def forward(u, slot, sem, to_s, to_r):
+        t, at = of(u)
+        remote(ag.at[slot, t, at], ag.at[slot, t, at], ag_s, sem, to_s, to_r).start()
+
+    def total(u):
+        t, at = of(u)
+
         @pl.when(is_middle)
         def _():
-            arrived(fm.at[t], in_r.at[t])
-            ag[p, t] = (up[t].astype(jnp.float32) + fm[t].astype(jnp.float32)).astype(jnp.bfloat16)
+            arrived(fm.at[t, at], in_r.at[u])
+            ag[p, t, at] = (up[t, at].astype(jnp.float32) + fm[t, at].astype(jnp.float32)).astype(jnp.bfloat16)
 
         @pl.when(jnp.logical_not(is_middle))
         def _():
-            arrived(ag.at[p, t], in_r.at[t])
+            arrived(ag.at[p, t, at], in_r.at[u])
 
         @pl.when(has_outer)
         def _():
-            remote(ag.at[p, t], ag.at[p, t], out_s, in_r.at[t], outer_s, r).start()
-
-    def close(t):
-        return t >= T - CLOSE_UNITS
-
-    def spread(t):
-        if close(t):
+            remote(ag.at[p, t, at], ag.at[p, t, at], out_s, in_r.at[u], outer_s, r).start()
+
+    def close(u):
+        return u >= U - CLOSE_PIECES
+
+    over_z = [t for t in OVER_Z if t < T and not close(t * PIECES + PIECES - 1)] if Z > 2 and R > 1 else []
+
+    def spread(u):
+        forward(u, p, rest_r, partner, r)
+        if close(u):
             for i in range(1, R):
-                forward(t, p, far_r.at[t], across, row_at(i))
-        forward(t, p, near_r.at[t], across, r)
-        for i in range(1, R):
-            forward(t, p, near_r.at[t], s, row_at(i))
-        forward(t, p, rest_r, partner, r)
-
-    def finish(t):
-        total(t)
-        spread(t)
+                forward(u, p, far_r.at[u], across, row_at(i))
+        ways = [(across, r)] + [(s, row_at(i)) for i in range(1, R)]
+        for (to_s, to_r), (other_s, other_r) in zip(ways, reversed(ways)):
+            forward(u, p, near_r.at[u], jnp.where(core == 0, to_s, other_s), jnp.where(core == 0, to_r, other_r))
+
+    def finish(u):
+        total(u)
+        spread(u)
 
     def climb_and_finish(t):
-        climb(t, 0)
-        if t >= SWAP_LAG:
-            @pl.when(is_middle)
-            def _():
-                finish(t - SWAP_LAG)
+        for u in range(t * PIECES, (t + 1) * PIECES):
+            climb(u)
+            if u >= SWAP_LAG:
+                pl.when(is_middle)(functools.partial(finish, u - SWAP_LAG))
 
     other = member(x, r, 1 - core)
     if T == PANELS:
-        low, high = halves(*product(panel(here), panel(here + PANELS // 2)))
+        low, high = halves(*product(turned(here), panel(here + PANELS // 2)))
         give(0, jnp.where(core == 0, high, low))
         own[0] = jnp.where(core == 0, low, high)
-        a = panel(other)
-        give(1, packed(*product(a, a)))
+        a, b = turned(other), turned(p)
+        give(1, packed(*product(a, panel(other))))
+        own[1] = packed(*product(b, panel(p)))
         for d in range(1, PANELS // 2):
             low, high = halves(*product(a, panel(lax.rem(other + d, PANELS))))
             give(2 * d, low)
             give(2 * d + 1, high)
-        climb_and_finish(0)
-        a = panel(p)
-        own[1] = packed(*product(a, a))
-        climb_and_finish(1)
-        for d in range(1, PANELS // 2):
-            own[2 * d], own[2 * d + 1] = halves(*product(a, panel(lax.rem(p + d, PANELS))))
-            climb_and_finish(2 * d)
-            climb_and_finish(2 * d + 1)
+            climb_and_finish(2 * d - 2)
+            climb_and_finish(2 * d - 1)
+            own[2 * d], own[2 * d + 1] = halves(*product(b, panel(lax.rem(p + d, PANELS))))
+        climb_and_finish(T - 2)
+        climb_and_finish(T - 1)
     else:
         def unit(n):
             kind, k, q, half = unit_place(n)
-            re, im = product(panel(k), panel(q))
+            re, im = product(turned(k), panel(q))
             low, high = halves(re, im)
             return jnp.where(kind == 1, packed(re, im), jnp.where(half == 0, low, high))
 
@@ -332,31 +345,43 @@
         for t in range(T):
             climb_and_finish(t)
 
-    def relay(t):
-        arrived(ag.at[pl.ds(0, R), t], near_r.at[t])
+    def relay(u):
+        t, at = of(u)
+        arrived(ag.at[pl.ds(0, R), t, at], near_r.at[u])
+        forward(u, member(1 - x, r, core), rest_r, partner, r)
+        for i in range(1, R):
+            forward(u, member(x, row_at(-i), core), rest_r, partner, r)
         first = core == 0
-        for i in range(1, R if not close(t) else 1):
-            slot = jnp.where(first, member(1 - x, r, core), member(x, row_at(-i), core))
-            forward(t, slot, far_r.at[t], jnp.where(first, s, across), jnp.where(first, row_at(i), r))
-        forward(t, member(1 - x, r, core), rest_r, partner, r)
+
+        def to_diagonal():
+            for i in range(1, R):
+                slot = jnp.where(first, member(1 - x, r, core), member(x, row_at(-i), core))
+                forward(u, slot, far_r.at[u], jnp.where(first, s, across), jnp.where(first, row_at(i), r))
+
+        if t in over_z:
+            pl.when(has_outer)(to_diagonal)
+        elif not close(u):
+            to_diagonal()
+
+    def diagonal(u):
+        t, at = of(u)
+        arrived(ag.at[pl.ds(0, R - 1), t, at], far_r.at[u])
         for i in range(1, R):
-            forward(t, member(x, row_at(-i), core), rest_r, partner, r)
-
-    def diagonal(t):
-        arrived(ag.at[pl.ds(0, R - 1), t], far_r.at[t])
-        for i in range(1, R):
-            forward(t, member(1 - x, row_at(-i), core), rest_r, partner, r)
-
-    for n in range(T + DIAGONAL_LAG):
-        if n < T - SWAP_LAG:
-            @pl.when(jnp.logical_not(is_middle))
-            def _():
-                finish(n)
-        elif n < T:
+            slot = member(1 - x, row_at(-i), core)
+            if t in over_z:
+                @pl.when(from_end == 1)
+                def _():
+                    remote(ag.at[slot, t, at], ag.at[slot, t, at], over_s, far_r.at[u], outer_s, r).start()
+            forward(u, slot, rest_r, partner, r)
+
+    for n in range(U + DIAGONAL_LAG):
+        if n < U - SWAP_LAG:
+            pl.when(jnp.logical_not(is_middle))(functools.partial(finish, n))
+        elif n < U:
             finish(n)
-        if 0 <= n - RELAY_LAG < T:
+        if 0 <= n - RELAY_LAG < U:
             relay(n - RELAY_LAG)
-        if 0 <= n - DIAGONAL_LAG < T:
+        if 0 <= n - DIAGONAL_LAG < U:
             diagonal(n - DIAGONAL_LAG)
     arrived(ag.at[pl.ds(0, slots)], rest_r)
 
@@ -370,7 +395,18 @@
     def _():
         left(up, out_s)
 
-    left(ag.at[pl.ds(0, G - 1)], ag_s)
+    left(ag.at[pl.ds(0, G - 1), pl.ds(0, T - len(over_z))], ag_s)
+    if over_z:
+        left(ag.at[pl.ds(0, G - R), pl.ds(0, len(over_z))], ag_s)
+        few = ag.at[pl.ds(0, R - 1), pl.ds(0, len(over_z))]
+
+        @pl.when(has_outer)
+        def _():
+            left(few, ag_s)
+
+        @pl.when(from_end == 1)
+        def _():
+            left(few, over_s)
 
 
 def expand(T, m_in, ag_ref, m_out, re_out, im_out, re_buf, im_buf, sems, m_sem):
@@ -463,9 +499,9 @@
             pltpu.VMEM(unit, bf), pltpu.VMEM(unit, bf), pltpu.VMEM(unit, bf),
             pltpu.VMEM(unit, bf), pltpu.VMEM(unit, bf),
             dma((2,)),
-            dma, dma((chunks,)), dma, dma((chunks,)), dma, dma,
-            dma, dma((T,)), dma, dma((T,)), dma, dma((T,)),
-            dma, dma((T,)), dma((T,)), dma,
+            dma, dma((chunks, 2)), dma, dma((chunks,)), dma, dma,
+            dma, dma((T,)), dma, dma((T * PIECES,)), dma, dma((T * PIECES,)),
+            dma, dma((T * PIECES,)), dma((T * PIECES,)), dma, dma,
         ],
         compiler_params=pltpu.CompilerParams(
             collective_id=0, has_side_effects=True, vmem_limit_bytes=32 * 2**20

time: 63.1 us -> 62.5 us (level)
  no operation moved by 1% of the time
where the time goes in v5:
time: 62.5 us; the launch traced here: 62.3 us
  Pallas kernels  61.7 us (99%)
  between operations  0.64 us (1%)
    pallas_call x1, Pallas kernels, local(): pl.pallas_call(functools.partial(exchange, N, R, rows, part, T, factor),...  58 us
    pallas_call x1, Pallas kernels, local(): pl.pallas_call(functools.partial(expand, T), out_shape=(jax.ShapeDtypeStr...  3.69 us

profile of v5, /device:TPU:0, one launch (start us, length us, event | category | flops | bytes accessed | tf_op | source)
XLA Modules:
  0.0 62.3 jit_solution(10085202564484376683)
XLA Ops:
  0.6 58.0 %shard_map.49 = (bf16[16,64,128]{2,1,0:T(8,128)(2,1)S(1)}, bf16[8,8,64,256]{3,2,1,0:T(8,128)(2,1)S(1)}) custom-call(f32[1024]{0:T(1024)} %constant.2.clone.w_hbm, bf16[4,1024,128]{2,1,0:T(8,128)(2,1)} %bitcast.2), custom_call_target="tpu_custom_call" | custom-call | flops 1000000000 | bytes 8388608 | tf_op jit(solution)/shard_map/pallas_call | solution.py:485
  58.6 3.7 %shard_map.50 = (bf16[16,64,128]{2,1,0:T(8,128)(2,1)}, f32[1024,1024]{1,0:T(8,128)}, f32[1024,1024]{1,0:T(8,128)}) custom-call(bf16[16,64,128]{2,1,0:T(8,128)(2,1)S(1)} %get-tuple-element.8.m_in, bf16[8,8,64,256]{3,2,1,0:T(8,128)(2,1)S(1)} %get-tuple-element.9.ag_ref), custom_call_target="tpu_custom_call" | custom-call | flops 10000000 | bytes 16777216 | tf_op jit(solution)/shard_map/pallas_call | solution.py:516

commit v6 on v5

--- a/solution.py
+++ b/solution.py
@@ -14,7 +14,6 @@
 OUTS = 2 * PANELS
 CHUNK_ROWS = 16
 LEAD = 2
-DIRECT = 2
 PIECES = 2
 CLOSE_PIECES = 4
 SWAP_LAG = 8
@@ -56,7 +55,7 @@
     N, R, rows, part, T, factor,
     w_hbm, x_hbm, m_ref, ag,
     w_ref, x_ref, xs, sbuf, own, dout, din, fo, up, fm,
-    in_sems, a2a_s, a2a_r, sg_s, sg_x, sg_r, sg_last, dd_s, dd_r, up_s, fo_r, out_s, in_r, ag_s, near_r, far_r, rest_r, over_s,
+    in_sems, a2a_s, a2a_r, sg_s, sg_r, dd_s, dd_r, up_s, fo_r, out_s, in_r, ag_s, near_r, far_r, rest_r, over_s,
 ):
     Z = N // 4
     CH = rows // part
@@ -151,7 +150,7 @@
     def panels_to(h, slot, sem, to_s, to_r):
         remote(sbuf.at[h, slot], sbuf.at[h, slot], sg_s, sem, to_s, to_r).start()
 
-    def moments_of(h, c, direct):
+    def moments_of(h, c):
         acc = weigh(None, [x_ref[q, rows_of(s, h), :] for q in range(inputs)], s)
         arrived(xs.at[h, pl.ds(0, N // 2)], a2a_r.at[h, 0])
 
@@ -171,34 +170,18 @@
             value = acc[o].astype(jnp.bfloat16)
             sbuf[h, here, o] = value
             m_ref[o, at, :] = value
-        if direct:
-            for i in range(1, R):
-                panels_to(h, here, sg_r, across, row_at(i))
-        panels_to(h, here, sg_last if direct else sg_x.at[h], across, r)
+        for i in range(1, R):
+            panels_to(h, here, sg_r, across, row_at(i))
+        panels_to(h, here, sg_r, across, r)
         for i in range(1, R):
             panels_to(h, here, sg_r, s, row_at(i))
 
-    def relay_panels(h):
-        slot = r * 2 + 1 - x
-        arrived(sbuf.at[h, slot], sg_x.at[h])
-        for i in range(1, R):
-            panels_to(h, slot, sg_r, s, row_at(i))
-
-    def moments_and_relay(h, c):
-        moments_of(h, c, False)
-        relay_panels(h)
+    def moments_direct(h, c):
+        moments_of(h, c)
         return c
 
-    last = max(CH - DIRECT, 0)
-    lax.fori_loop(0, last, moments_and_relay, 0)
-
-    def moments_direct(h, c):
-        moments_of(h, c, True)
-        return c
-
-    lax.fori_loop(last, CH, moments_direct, 0)
-    arrived(sbuf.at[pl.ds(last, CH - last), 0], sg_last)
-    arrived(sbuf.at[:, pl.ds(0, slots - 2)], sg_r)
+    lax.fori_loop(0, CH, moments_direct, 0)
+    arrived(sbuf.at[:, pl.ds(0, slots - 1)], sg_r)
 
 
     depth = slots * rows
@@ -499,7 +482,7 @@
             pltpu.VMEM(unit, bf), pltpu.VMEM(unit, bf), pltpu.VMEM(unit, bf),
             pltpu.VMEM(unit, bf), pltpu.VMEM(unit, bf),
             dma((2,)),
-            dma, dma((chunks, 2)), dma, dma((chunks,)), dma, dma,
+            dma, dma((chunks, 2)), dma, dma,
             dma, dma((T,)), dma, dma((T * PIECES,)), dma, dma((T * PIECES,)),
             dma, dma((T * PIECES,)), dma((T * PIECES,)), dma, dma,
         ],

time: 62.5 us -> 62.3 us (level)
  no operation moved by 1% of the time
where the time goes in v6:
time: 62.3 us; the launch traced here: 62.2 us
  Pallas kernels  61.5 us (99%)
  between operations  0.64 us (1%)
    pallas_call x1, Pallas kernels, local(): pl.pallas_call(functools.partial(exchange, N, R, rows, part, T, factor),...  57.8 us
    pallas_call x1, Pallas kernels, local(): pl.pallas_call(functools.partial(expand, T), out_shape=(jax.ShapeDtypeStr...  3.69 us

profile of v6, /device:TPU:0, one launch (start us, length us, event | category | flops | bytes accessed | tf_op | source)
XLA Modules:
  0.0 62.2 jit_solution(1015460708358032541)
XLA Ops:
  0.6 57.8 %shard_map.49 = (bf16[16,64,128]{2,1,0:T(8,128)(2,1)S(1)}, bf16[8,8,64,256]{3,2,1,0:T(8,128)(2,1)S(1)}) custom-call(f32[1024]{0:T(1024)} %constant.2.clone.w_hbm, bf16[4,1024,128]{2,1,0:T(8,128)(2,1)} %bitcast.2), custom_call_target="tpu_custom_call" | custom-call | flops 1000000000 | bytes 8388608 | tf_op jit(solution)/shard_map/pallas_call | solution.py:468
  58.5 3.7 %shard_map.50 = (bf16[16,64,128]{2,1,0:T(8,128)(2,1)}, f32[1024,1024]{1,0:T(8,128)}, f32[1024,1024]{1,0:T(8,128)}) custom-call(bf16[16,64,128]{2,1,0:T(8,128)(2,1)S(1)} %get-tuple-element.8.m_in, bf16[8,8,64,256]{3,2,1,0:T(8,128)(2,1)S(1)} %get-tuple-element.9.ag_ref), custom_call_target="tpu_custom_call" | custom-call | flops 10000000 | bytes 16777216 | tf_op jit(solution)/shard_map/pallas_call | solution.py:499
